TPU v7x, 32 devices: a whole 2x2x4 slice. The times are simulated.
32 devices in a mesh: seq: 8 (over z, y), rep: 4 (over x, core).
Axes of the slice: x: 2, y: 2, z: 4, core: 2. Of those that a mesh axis runs over, the one named last changes fastest.
Arguments:
- inputs: bfloat16 [4, 1024, 1024], P('rep', 'seq'), may hold values from -6 to 6
- weight_t: bfloat16 [3072, 1024], P('seq', 'rep'), may hold values from -0.1875 to 0.1875
- states: float32 [4, 1024, 1024], P('rep', 'seq'), may hold values from -0.9 to 0.9
- doc_ids: int32 [4, 1024], P('rep', 'seq'), may hold values from 0 to 3, never falling along the last dimension, each value on 1 to 512 neighbouring positions
- recur: float32 [3, 1024], replicated, may hold values from -1 to 1
- bias: float32 [3, 1024], replicated, may hold values from -8 to 3, as said below
- out_grad: bfloat16 [4, 1024, 1024], P('rep', 'seq'), may hold values from -6 to 6
Outputs:
- input_grad: bfloat16 [4, 1024, 1024], P('rep', 'seq')
- weight_grad: float32 [3072, 1024], P('seq', 'rep')
- param_grad: float32 [6, 1024], replicated
Inputs may be any that keep to these rules, and one draw needn't show every extreme that they name: `doc_ids`: within each sequence the numbers never fall; every document has 1 to 512 tokens, and some document has exactly 512. `bias`: row 0 lies between -8 and -1, rows 1 and 2 between -3 and 3.
All inputs are finite; a program needn't handle non-finite values.
Results may differ from a plain program's by a relative error of at most 0.0095.
Values may be sent and summed in bfloat16 or wider, within the bound.
A program may use at most 128 MiB of HBM per device.

v0:
```python
import math
import jax
import jax.numpy as jnp
from jax import lax
from jax.sharding import PartitionSpec as P


def shifted(block, axis, distance):
    devices = range(lax.axis_size(axis))
    route = [(i - distance, i) for i in devices if i - distance in devices]
    return lax.ppermute(block, axis, route)


def compose(earlier, later):
    return (later[0] * earlier[0], later[1] + later[0] * earlier[1])


def local(inputs, weight_t, states, doc_ids, recur, bias, out_grad):
    feats = inputs[0]
    hidden_now = states[0]
    ids_float = doc_ids[0].astype(jnp.float32)
    count = feats.shape[0]
    width = hidden_now.shape[1]
    columns = lax.all_gather(weight_t, "rep", axis=1, tiled=True)
    contract_last = (((1,), (1,)), ((), ()))
    full_weight = lax.all_gather(columns, "seq", axis=0, tiled=True)
    preact = lax.dot_general(feats, full_weight, contract_last, preferred_element_type=jnp.float32)
    tail_state, tail_id = shifted((hidden_now[-1:], ids_float[-1:]), "seq", 1)
    first_same = jnp.where(
        (ids_float[0] == tail_id[0]) & (lax.axis_index("seq") > 0), 1.0, 0.0
    ).astype(jnp.float32)
    same = jnp.concatenate(
        [first_same[None], (ids_float[1:] == ids_float[:-1]).astype(jnp.float32)]
    )
    prior = jnp.concatenate([tail_state, hidden_now[:-1]], 0) * same[:, None]
    gate_z = jax.nn.sigmoid(preact[:, :width] + recur[0] * prior + bias[0])
    gate_r = jax.nn.sigmoid(preact[:, width : 2 * width] + recur[1] * prior + bias[1])
    gate_c = jnp.tanh(preact[:, 2 * width :] + recur[2] * gate_r * prior + bias[2])
    jacobian = same[:, None] * (
        1.0
        - gate_z
        + (gate_c - prior) * gate_z * (1.0 - gate_z) * recur[0]
        + gate_z
        * (1.0 - gate_c * gate_c)
        * recur[2]
        * (gate_r + prior * gate_r * (1.0 - gate_r) * recur[1])
    )
    upstream = out_grad[0].astype(jnp.float32)
    jac_rows, up_rows = (
        lax.all_to_all(jacobian.T, "seq", split_axis=0, concat_axis=1, tiled=True),
        lax.all_to_all(upstream.T, "seq", split_axis=0, concat_axis=1, tiled=True),
    )
    factor = jnp.concatenate([jac_rows[:, 1:], jnp.zeros((jac_rows.shape[0], 1), jnp.float32)], 1)
    _, adjoint_rows = lax.associative_scan(compose, (factor, up_rows), reverse=True, axis=1)
    adjoint = lax.all_to_all(adjoint_rows, "seq", split_axis=1, concat_axis=0, tiled=True).T
    grad_z = adjoint * (gate_c - prior) * gate_z * (1.0 - gate_z)
    grad_c = adjoint * gate_z * (1.0 - gate_c * gate_c)
    grad_r = grad_c * recur[2] * prior * gate_r * (1.0 - gate_r)
    grad_pre = jnp.concatenate([grad_z, grad_r, grad_c], 1).astype(jnp.bfloat16)
    input_grad = jnp.dot(grad_pre, full_weight, preferred_element_type=jnp.float32)
    tokens_all = count * inputs.shape[0] * lax.axis_size("seq") * lax.axis_size("rep")
    normal_factor = 1.0 / math.sqrt(tokens_all)
    row_share = lax.psum_scatter(
        lax.dot_general(
            grad_pre, feats, (((0,), (0,)), ((), ())), preferred_element_type=jnp.float32
        ),
        "seq",
        scatter_dimension=0,
        tiled=True,
    )
    weight_grad = (
        lax.psum_scatter(
            row_share.astype(jnp.bfloat16), "rep", scatter_dimension=1, tiled=True
        ).astype(jnp.float32)
        * normal_factor
    )
    stats = jnp.stack(
        [
            grad_z.sum(0),
            grad_r.sum(0),
            grad_c.sum(0),
            (grad_z * prior).sum(0),
            (grad_r * prior).sum(0),
            (grad_c * gate_r * prior).sum(0),
        ]
    )
    param_grad = lax.psum(stats, ("seq", "rep")) * normal_factor
    return (input_grad.astype(jnp.bfloat16)[None], weight_grad, param_grad)


def solution(mesh):
    placed = (
        P("rep", "seq", None),
        P("seq", "rep"),
        P("rep", "seq", None),
        P("rep", "seq"),
        P(),
        P(),
        P("rep", "seq", None),
    )
    return jax.shard_map(
        local,
        mesh=mesh,
        in_specs=placed,
        out_specs=(P("rep", "seq", None), P("seq", "rep"), P()),
        check_vma=False,
    )
```

profile of v0, /device:TPU:0, one launch (start us, length us, event | category | flops | bytes accessed | tf_op | source)
XLA Modules:
  0.0 491.4 jit_solution(18385137196122489823)
XLA Ops:
  7.3 11.8 %all_gather.6 = bf16[384,1024]{1,0:T(8,128)(2,1)} all-gather(bf16[384,256]{1,0:T(8,128)(2,1)} %param.8), channel_id=1, replica_groups=mesh['seq'=8,'rep'=4] {'rep'}, dimensions={1}, use_global_device_ids=true | all-gather | bytes 983040 | tf_op jit(solution)/shard_map/all_gather | solution.py:24
  19.7 4.0 collective-permute-start
  23.7 2.9 collective-permute-start.1
  26.8 0.9 bitcast_convert_fusion
  27.6 4.8 all-to-all-start
  34.1 95.4 %all-gather.2.cloned.1.call-done = bf16[3072,1024]{1,0:T(8,128)(2,1)} async-done(((bf16[384,1024]{1,0:T(8,128)(2,1)}), bf16[3072,1024]{1,0:T(8,128)(2,1)}) %all-gather.2.cloned.1.call-update) | async-done | bytes 6291472 | tf_op jit(solution)/shard_map/all_gather | solution.py:26
  129.5 5.0 %fusion.21 = f32[128,3072]{1,0:T(8,128)S(1)} fusion(bf16[3072,1024]{1,0:T(8,128)(2,1)} %all-gather.2.cloned.1.call-done, bf16[1,128,1024]{2,1,0:T(8,128)(2,1)S(1)} %copy-done), kind=kOutput, calls=%fused_computation.40 | convolution fusion | flops 805306368 | bytes 8126464 | tf_op jit(solution)/shard_map/dot_general | solution.py:27
  134.5 1.6 copy_bitcast_fusion
  136.1 4.2 all-to-all-start.1
  140.5 1.4 slice.317
  143.2 1.9 slice.318
  145.1 1.3 slice.342
  146.5 1.3 slice.346
  147.8 5.9 %all-to-all-done.1 = f32[8,128,128]{1,2,0:T(8,128)} async-done(((f32[8,128,128]{1,2,0:T(8,128)}), f32[8,128,128]{1,2,0:T(8,128)}, u32[]{:S(2)}, u32[]{:S(2)}) %all-to-all-start.1) | async-done | bytes 524320 | tf_op jit(solution)/shard_map/all_to_all | solution.py:50
  153.7 1.1 slice.421
  154.8 1.4 slice.339
  156.2 1.4 slice.343
  158.0 2.9 slice.344
  160.9 1.3 slice.350
  162.2 1.2 fusion.34
  163.5 0.7 slice.357
  164.2 0.7 slice.352
  164.9 0.7 slice.354
  165.6 1.1 fusion.35
  169.3 0.9 fusion.36
  171.5 0.8 fusion.37
  176.2 1.2 pad.65
  183.3 0.9 slice.351
  184.8 1.9 slice.340
  189.4 0.7 multiply_add_fusion.6
  190.8 0.7 fusion.27
  192.1 0.7 fusion.26
  193.5 0.8 fusion.25
  195.0 0.9 fusion.24
  196.6 0.9 pad.79
  197.6 0.9 fusion.23
  198.6 0.7 add.232
  199.4 1.0 pad.81
  200.6 0.9 add.234
  201.4 3.4 rev.2
  204.9 17.3 %all_to_all.63 = f32[128,8,128]{0,2,1:T(8,128)S(1)} all-to-all(f32[128,8,128]{0,2,1:T(8,128)S(1)} %bitcast.86), channel_id=1, replica_groups=mesh['seq'=8,'rep'=4] {'seq'}, dimensions={1} | all-to-all | bytes 1048576 | tf_op jit(solution)/shard_map/all_to_all | solution.py:55
  222.2 1.0 multiply_reduce_fusion
  223.1 6.3 %fusion.18 = f32[3072,1024]{1,0:T(8,128)} fusion(bf16[128,1024]{1,0:T(8,128)(2,1)S(1)} %get-tuple-element.11, bf16[128,1024]{1,0:T(8,128)(2,1)S(1)} %get-tuple-element.10, bf16[128,1024]{1,0:T(8,128)(2,1)S(1)} %get-tuple-element.9, bf16[1,128,1024]{2,1,0:T(8,128)(2,1)S(1)} %copy-done), kind=kOutput, calls=%fused_computation.34 | convolution fusion | flops 807665664 | bytes 13631488 | tf_op jit(solution)/shard_map/dot_general | solution.py:64
  229.6 206.6 %reduce-scatter.3.cloned.1.call-done = f32[384,1024]{1,0:T(8,128)} async-done(((f32[3072,1024]{1,0:T(8,128)}), f32[384,1024]{1,0:T(8,128)}) %reduce-scatter.3.cloned.1.call-update) | async-done | bytes 1572880 | tf_op jit(solution)/shard_map/reduce_scatter | solution.py:63
  436.1 2.4 convert_element_type.29
  438.6 39.5 %psum.7 = f32[6,1024]{1,0:T(8,128)S(1)} all-reduce(f32[6,1024]{1,0:T(8,128)S(1)} %stack.27), channel_id=1, replica_groups=mesh['seq'=8,'rep'=4] {'seq','rep'}, use_global_device_ids=true, to_apply=%region_8.9 | all-reduce | flops 6144 | bytes 49152 | tf_op jit(solution)/shard_map/psum | solution.py:87
  478.7 4.5 fusion
  483.2 1.7 convert_multiply_fusion
  (167 shorter events, 24.4 us)
Async XLA Ops:
  7.2 122.3 %copy-start = (bf16[1,128,1024]{2,1,0:T(8,128)(2,1)S(1)}, bf16[1,128,1024]{2,1,0:T(8,128)(2,1)}, u32[]{:S(2)}) copy-start(bf16[1,128,1024]{2,1,0:T(8,128)(2,1)} %param.7) | copy-start | bytes 786436
  7.2 11.9 %copy-start.24 = (s32[1,128]{1,0:T(1,128)S(1)}, s32[1,128]{1,0:T(1,128)}, u32[]{:S(2)}) copy-start(s32[1,128]{1,0:T(1,128)} %param.10) | copy-start | bytes 1540
  7.2 16.5 %copy-start.1 = (f32[1,128,1024]{2,1,0:T(8,128)S(1)}, f32[1,128,1024]{2,1,0:T(8,128)}, u32[]{:S(2)}) copy-start(f32[1,128,1024]{2,1,0:T(8,128)} %param.9) | copy-start | bytes 1572868
  7.2 19.4 %copy-start.2 = (bf16[1,128,1024]{2,1,0:T(8,128)(2,1)S(1)}, bf16[1,128,1024]{2,1,0:T(8,128)(2,1)}, u32[]{:S(2)}) copy-start(bf16[1,128,1024]{2,1,0:T(8,128)(2,1)} %param.13) | copy-start | bytes 786436
  7.2 122.2 %all-gather.2.cloned.1.call-start = ((), (), s32[]{:S(2)}) async-start(), calls=%async_computation.5 | async-start | bytes 7077888 | tf_op jit(solution)/shard_map/all_gather | solution.py:26
  19.1 13.4 %copy-start.17 = (f32[3,1024]{1,0:T(4,128)S(1)}, f32[3,1024]{1,0:T(4,128)}, u32[]{:S(2)}) copy-start(f32[3,1024]{1,0:T(4,128)} %param.12) | copy-start | bytes 36868
  19.1 13.4 %copy-start.18 = (f32[3,1024]{1,0:T(4,128)S(1)}, f32[3,1024]{1,0:T(4,128)}, u32[]{:S(2)}) copy-start(f32[3,1024]{1,0:T(4,128)} %param.11) | copy-start | bytes 36868
  19.7 13.0 %collective-permute-start = (f32[1]{0:T(128)}, f32[1]{0:T(128)}, u32[]{:S(2)}, u32[]{:S(2)}) collective-permute-start(f32[1]{0:T(128)} %bitcast.6), channel_id=1, source_target_pairs={{0,4},{4,8},{8,12},{12,16},{16,20},{20,24},{24,28},{1,5},{5,9},{9,... | collective-permute-start | bytes 20 | tf_op jit(solution)/shard_map/ppermute | solution.py:11
  23.7 110.7 %collective-permute-start.1 = (f32[1,1024]{1,0:T(1,128)S(1)}, f32[1,1024]{1,0:T(1,128)S(1)}, u32[]{:S(2)}, u32[]{:S(2)}) collective-permute-start(f32[1,1024]{1,0:T(1,128)S(1)} %slice_bitcast_fusion.1), channel_id=1, source_target_pairs={{0,4},{4,8},{8,12},{12,16},{16,20},{20,24},{24,28},{1,5},{5,9},{9,... | collective-permute-start | bytes 12296 | tf_op jit(solution)/shard_map/ppermute | solution.py:11
  27.6 108.5 %all-to-all-start = ((f32[8,128,128]{2,1,0:T(8,128)}), f32[8,128,128]{2,1,0:T(8,128)S(1)}, u32[]{:S(2)}, u32[]{:S(2)}) async-start(f32[8,128,128]{2,1,0:T(8,128)} %bitcast.2), calls=%async_computation | async-start | bytes 1048576 | tf_op jit(solution)/shard_map/all_to_all | solution.py:51
  32.5 101.9 %copy-start.3 = (f32[1,1024]{1,0:T(1,128)}, f32[1,1024]{1,0:T(1,128)S(1)}, u32[]{:S(2)}) copy-start(f32[1,1024]{1,0:T(1,128)S(1)} %get-tuple-element.25) | copy-start | bytes 12292
  32.5 101.9 %copy-start.5 = (f32[1,1024]{1,0:T(1,128)}, f32[1,1024]{1,0:T(1,128)S(1)}, u32[]{:S(2)}) copy-start(f32[1,1024]{1,0:T(1,128)S(1)} %get-tuple-element.26) | copy-start | bytes 12292
  32.5 101.9 %copy-start.7 = (f32[1,1024]{1,0:T(1,128)}, f32[1,1024]{1,0:T(1,128)S(1)}, u32[]{:S(2)}) copy-start(f32[1,1024]{1,0:T(1,128)S(1)} %get-tuple-element.27) | copy-start | bytes 12292
  32.6 101.9 %copy-start.9 = (f32[1,1024]{1,0:T(1,128)}, f32[1,1024]{1,0:T(1,128)S(1)}, u32[]{:S(2)}) copy-start(f32[1,1024]{1,0:T(1,128)S(1)} %get-tuple-element.22) | copy-start | bytes 12292
  32.6 101.9 %copy-start.11 = (f32[1,1024]{1,0:T(1,128)}, f32[1,1024]{1,0:T(1,128)S(1)}, u32[]{:S(2)}) copy-start(f32[1,1024]{1,0:T(1,128)S(1)} %get-tuple-element.23) | copy-start | bytes 12292
  32.6 101.9 %copy-start.13 = (f32[1,1024]{1,0:T(1,128)}, f32[1,1024]{1,0:T(1,128)S(1)}, u32[]{:S(2)}) copy-start(f32[1,1024]{1,0:T(1,128)S(1)} %get-tuple-element.24) | copy-start | bytes 12292
  34.1 100.5 %copy-start.19 = (f32[128]{0:T(128)}, f32[128]{0:T(128)S(1)}, u32[]{:S(2)}) copy-start(f32[128]{0:T(128)S(1)} %pad_maximum_fusion.12) | copy-start | bytes 1540
  134.4 1.7 copy-start.15
  136.1 17.6 %all-to-all-start.1 = ((f32[8,128,128]{1,2,0:T(8,128)}), f32[8,128,128]{1,2,0:T(8,128)}, u32[]{:S(2)}, u32[]{:S(2)}) async-start(f32[8,128,128]{1,2,0:T(8,128)} %copy_bitcast_fusion), calls=%async_computation.1 | async-start | bytes 1048576 | tf_op jit(solution)/shard_map/all_to_all | solution.py:50
  140.3 295.8 %reduce-scatter.3.cloned.1.call-start = ((), (), s32[]{:S(2)}) async-start(), calls=%async_computation.6 | async-start | bytes 14155776 | tf_op jit(solution)/shard_map/reduce_scatter | solution.py:63
  184.2 11.7 %copy-start.23 = (f32[128,1]{0,1:T(1,128)S(1)}, f32[128,1]{0,1:T(1,128)}, u32[]{:S(2)}) copy-start(f32[128,1]{0,1:T(1,128)} %slice.423) | copy-start | bytes 1540
  192.9 5.6 %copy-start.22 = (f32[128,1]{0,1:T(1,128)S(1)}, f32[128,1]{0,1:T(1,128)}, u32[]{:S(2)}) copy-start(f32[128,1]{0,1:T(1,128)} %slice.422) | copy-start | bytes 1540
  197.5 1.8 copy-start.21
  200.5 21.6 %copy-start.4 = (f32[1,1024]{1,0:T(1,128)S(1)}, f32[1,1024]{1,0:T(1,128)}, u32[]{:S(2)}) copy-start(f32[1,1024]{1,0:T(1,128)} %copy-done.3) | copy-start | bytes 12292
  200.5 21.6 %copy-start.6 = (f32[1,1024]{1,0:T(1,128)S(1)}, f32[1,1024]{1,0:T(1,128)}, u32[]{:S(2)}) copy-start(f32[1,1024]{1,0:T(1,128)} %copy-done.5) | copy-start | bytes 12292
  200.5 21.6 %copy-start.8 = (f32[1,1024]{1,0:T(1,128)S(1)}, f32[1,1024]{1,0:T(1,128)}, u32[]{:S(2)}) copy-start(f32[1,1024]{1,0:T(1,128)} %copy-done.7) | copy-start | bytes 12292
  200.5 21.6 %copy-start.10 = (f32[1,1024]{1,0:T(1,128)S(1)}, f32[1,1024]{1,0:T(1,128)}, u32[]{:S(2)}) copy-start(f32[1,1024]{1,0:T(1,128)} %copy-done.9) | copy-start | bytes 12292
  200.5 21.6 %copy-start.12 = (f32[1,1024]{1,0:T(1,128)S(1)}, f32[1,1024]{1,0:T(1,128)}, u32[]{:S(2)}) copy-start(f32[1,1024]{1,0:T(1,128)} %copy-done.11) | copy-start | bytes 12292
  200.5 21.6 %copy-start.14 = (f32[1,1024]{1,0:T(1,128)S(1)}, f32[1,1024]{1,0:T(1,128)}, u32[]{:S(2)}) copy-start(f32[1,1024]{1,0:T(1,128)} %copy-done.13) | copy-start | bytes 12292
  200.5 21.6 %copy-start.16 = (f32[1,1024]{1,0:T(1,128)S(1)}, f32[1,1024]{1,0:T(1,128)}, u32[]{:S(2)}) copy-start(f32[1,1024]{1,0:T(1,128)} %copy-done.15) | copy-start | bytes 12292
  200.6 21.6 %copy-start.20 = (f32[128]{0:T(128)S(1)}, f32[128]{0:T(128)}, u32[]{:S(2)}) copy-start(f32[128]{0:T(128)} %copy-done.19) | copy-start | bytes 1540
  229.5 253.7 %reduce-scatter.5.cloned.1.call-start = ((), (), s32[]{:S(2)}) async-start(), calls=%async_computation.7 | async-start | bytes 983040 | tf_op jit(solution)/shard_map/reduce_scatter | solution.py:72
Sparse Core Ops, SparseCore 0:
  19.2 110.1 all-gather.1
  229.6 206.4 reduce-scatter.2
  438.7 22.3 reduce-scatter.4
where the time goes:
time: 493 us; the launch traced here: 491 us
  waiting for transfers between devices  308 us (62%)
  blocking collectives  68.6 us (14%)
  local copies, waits for them, and re-layouts  42.2 us (9%)
  other arithmetic  25.3 us (5%)
  starting transfers between devices  16 us (3%)
  matrix products  15.8 us (3%)
  between operations  15.7 us (3%)
    reduce_scatter x1, waiting for transfers between devices, local(): lax.psum_scatter(lax.dot_general(grad_pre, feats, (((0,), (0,)), ((), ())...  207 us
    all_gather x1, waiting for transfers between devices, local(): full_weight = lax.all_gather(columns, 'seq', axis=0, tiled=True)  95.4 us
    psum x1, blocking collectives, local(): param_grad = lax.psum(stats, ('seq', 'rep')) * normal_factor  39.5 us
    slice x66, local copies, waits for them, and re-layouts, local(): lax.associative_scan(compose, (factor, up_rows), reverse=True, axis=1)  33.1 us
    all_to_all x1, blocking collectives, local(): lax.all_to_all(adjoint_rows, 'seq', split_axis=1, concat_axis=0, tiled=True)  17.3 us
    all_gather x1, blocking collectives, local(): columns = lax.all_gather(weight_t, 'rep', axis=1, tiled=True)  11.8 us
  transfers between devices with their start and end apart: 7, of which 3 were waited for; matrix products, arithmetic and copies ran while one was open for 4% of the time, Pallas kernels for 0%

commit v1 on v0

--- a/solution.py
+++ b/solution.py
@@ -23,7 +23,10 @@
     width = hidden_now.shape[1]
     columns = lax.all_gather(weight_t, "rep", axis=1, tiled=True)
     contract_last = (((1,), (1,)), ((), ()))
-    full_weight = lax.all_gather(columns, "seq", axis=0, tiled=True)
+    n_dev = lax.axis_size("seq")
+    blocks = jnp.stack([columns for _ in range(n_dev)])
+    blocks = lax.all_to_all(blocks, "seq", split_axis=0, concat_axis=0)
+    full_weight = jnp.concatenate(blocks, axis=0)
     preact = lax.dot_general(feats, full_weight, contract_last, preferred_element_type=jnp.float32)
     tail_state, tail_id = shifted((hidden_now[-1:], ids_float[-1:]), "seq", 1)
     first_same = jnp.where(

time: 493 us -> 543 us (1.10)
  waiting for transfers between devices: 308 us -> 349 us
    all_to_all x0 -> x1, waiting for transfers between devices: none -> 130 us  [local(): blocks = lax.all_to_all(blocks, 'seq', split_axis=0, concat_axis=0)]
    all_gather x1 -> x0, waiting for transfers between devices: 95.4 us -> none  [local(): full_weight = lax.all_gather(columns, 'seq', axis=0, tiled=True)]
    all_to_all x1, waiting for transfers between devices: 0.01 us -> 6.55 us  [local(): lax.all_to_all(upstream.T, 'seq', split_axis=0, concat_axis=1, tiled=True)]
    all_to_all x0 -> x1, starting transfers between devices: none -> 5.98 us  [local(): blocks = lax.all_to_all(blocks, 'seq', split_axis=0, concat_axis=0)]
  transfers between devices with their start and end apart: 7 -> 7, of which waited for: 3 -> 4; matrix products, arithmetic and copies ran while one was open for 4% -> 4% of each run, Pallas kernels for 0% -> 0%
where the time goes in v1:
time: 543 us; the launch traced here: 541 us
  waiting for transfers between devices  349 us (64%)
  blocking collectives  67.9 us (13%)
  local copies, waits for them, and re-layouts  45.8 us (8%)
  other arithmetic  25.4 us (5%)
  starting transfers between devices  21.2 us (4%)
  between operations  16 us (3%)
  matrix products  15.8 us (3%)
    reduce_scatter x1, waiting for transfers between devices, local(): lax.psum_scatter(lax.dot_general(grad_pre, feats, (((0,), (0,)), ((), ())...  206 us
    all_to_all x1, waiting for transfers between devices, local(): blocks = lax.all_to_all(blocks, 'seq', split_axis=0, concat_axis=0)  130 us
    psum x1, blocking collectives, local(): param_grad = lax.psum(stats, ('seq', 'rep')) * normal_factor  39.4 us
    slice x66, local copies, waits for them, and re-layouts, local(): lax.associative_scan(compose, (factor, up_rows), reverse=True, axis=1)  33.3 us
    all_to_all x1, blocking collectives, local(): lax.all_to_all(adjoint_rows, 'seq', split_axis=1, concat_axis=0, tiled=True)  18 us
  transfers between devices with their start and end apart: 7, of which 4 were waited for; matrix products, arithmetic and copies ran while one was open for 4% of the time, Pallas kernels for 0%

profile of v1, /device:TPU:0, one launch (start us, length us, event | category | flops | bytes accessed | tf_op | source)
XLA Modules:
  0.0 541.3 jit_solution(16782280125979112429)
XLA Ops:
  7.2 10.4 %all_gather.3 = bf16[384,1024]{1,0:T(8,128)(2,1)S(1)} all-gather(bf16[384,256]{1,0:T(8,128)(2,1)} %param.8), channel_id=1, replica_groups=mesh['seq'=8,'rep'=4] {'rep'}, dimensions={1}, use_global_device_ids=true | all-gather | bytes 983040 | tf_op jit(solution)/shard_map/all_gather | solution.py:24
  17.6 3.5 stack.32
  21.1 6.0 %all-to-all-start.1 = ((bf16[8,384,1024]{2,1,0:T(8,128)(2,1)}), bf16[8,384,1024]{2,1,0:T(8,128)(2,1)}, u32[]{:S(2)}, u32[]{:S(2)}) async-start(bf16[8,384,1024]{2,1,0:T(8,128)(2,1)} %stack.32), calls=%async_computation.1 | async-start | bytes 12582912 | tf_op jit(solution)/shard_map/all_to_all | solution.py:28
  27.7 4.5 collective-permute-start
  32.1 2.8 collective-permute-start.1
  35.3 0.8 bitcast_convert_fusion
  36.2 129.6 %all-to-all-done.1 = bf16[8,384,1024]{2,1,0:T(8,128)(2,1)} async-done(((bf16[8,384,1024]{2,1,0:T(8,128)(2,1)}), bf16[8,384,1024]{2,1,0:T(8,128)(2,1)}, u32[]{:S(2)}, u32[]{:S(2)}) %all-to-all-start.1) | async-done | bytes 6291488 | tf_op jit(solution)/shard_map/all_to_all | solution.py:28
  165.8 3.7 all-to-all-start
  170.9 5.0 fusion.21
  176.0 1.6 copy_bitcast_fusion
  177.6 6.5 %all-to-all-done = f32[8,128,128]{2,1,0:T(8,128)S(1)} async-done(((f32[8,128,128]{2,1,0:T(8,128)}), f32[8,128,128]{2,1,0:T(8,128)S(1)}, u32[]{:S(2)}, u32[]{:S(2)}) %all-to-all-start) | async-done | bytes 524320 | tf_op jit(solution)/shard_map/all_to_all | solution.py:54
  184.1 4.1 all-to-all-start.2
  188.5 1.4 slice.317
  191.2 1.9 slice.318
  193.1 1.3 slice.342
  194.4 1.3 slice.346
  195.7 6.8 %all-to-all-done.2 = f32[8,128,128]{1,2,0:T(8,128)} async-done(((f32[8,128,128]{1,2,0:T(8,128)}), f32[8,128,128]{1,2,0:T(8,128)}, u32[]{:S(2)}, u32[]{:S(2)}) %all-to-all-start.2) | async-done | bytes 524320 | tf_op jit(solution)/shard_map/all_to_all | solution.py:53
  202.5 1.1 slice.421
  203.7 1.4 slice.339
  205.0 1.4 slice.343
  206.8 2.9 slice.344
  209.7 1.3 slice.350
  211.0 1.2 fusion.34
  212.4 0.7 slice.357
  214.4 1.1 fusion.35
  218.1 0.9 fusion.36
  220.3 0.8 fusion.37
  225.0 1.2 pad.65
  232.3 0.9 slice.351
  233.8 1.9 slice.340
  239.8 0.7 fusion.27
  241.2 0.7 fusion.26
  242.7 0.8 fusion.25
  244.2 0.9 fusion.24
  245.8 0.9 pad.79
  246.8 0.9 fusion.23
  247.8 0.7 add.232
  248.7 1.0 pad.81
  249.8 0.9 add.234
  250.6 3.4 rev.2
  254.1 18.0 %all_to_all.68 = f32[128,8,128]{0,2,1:T(8,128)S(1)} all-to-all(f32[128,8,128]{0,2,1:T(8,128)S(1)} %bitcast.87), channel_id=1, replica_groups=mesh['seq'=8,'rep'=4] {'seq'}, dimensions={1} | all-to-all | bytes 1048576 | tf_op jit(solution)/shard_map/all_to_all | solution.py:58
  272.1 1.0 multiply_reduce_fusion
  273.1 6.4 %fusion.18 = f32[3072,1024]{1,0:T(8,128)} fusion(bf16[128,1024]{1,0:T(8,128)(2,1)S(1)} %get-tuple-element.11, bf16[128,1024]{1,0:T(8,128)(2,1)S(1)} %get-tuple-element.10, bf16[128,1024]{1,0:T(8,128)(2,1)S(1)} %get-tuple-element.9, bf16[1,128,1024]{2,1,0:T(8,128)(2,1)S(1)} %copy-done), kind=kOutput, calls=%fused_computation.34 | convolution fusion | flops 807665664 | bytes 13631488 | tf_op jit(solution)/shard_map/dot_general | solution.py:67
  279.5 206.2 %reduce-scatter.3.cloned.1.call-done = f32[384,1024]{1,0:T(8,128)} async-done(((f32[3072,1024]{1,0:T(8,128)}), f32[384,1024]{1,0:T(8,128)}) %reduce-scatter.3.cloned.1.call-update) | async-done | bytes 1572880 | tf_op jit(solution)/shard_map/reduce_scatter | solution.py:66
  485.7 2.4 convert_element_type.29
  488.2 39.4 %psum.7 = f32[6,1024]{1,0:T(8,128)S(1)} all-reduce(f32[6,1024]{1,0:T(8,128)S(1)} %stack.39), channel_id=1, replica_groups=mesh['seq'=8,'rep'=4] {'seq','rep'}, use_global_device_ids=true, to_apply=%region_8.9 | all-reduce | flops 6144 | bytes 49152 | tf_op jit(solution)/shard_map/psum | solution.py:90
  528.3 4.5 fusion
  532.8 1.7 convert_multiply_fusion
  (167 shorter events, 26.8 us)
Async XLA Ops:
  7.2 163.8 %copy-start = (bf16[1,128,1024]{2,1,0:T(8,128)(2,1)S(1)}, bf16[1,128,1024]{2,1,0:T(8,128)(2,1)}, u32[]{:S(2)}) copy-start(bf16[1,128,1024]{2,1,0:T(8,128)(2,1)} %param.7) | copy-start | bytes 786436
  21.1 6.0 %copy-start.24 = (s32[1,128]{1,0:T(1,128)S(1)}, s32[1,128]{1,0:T(1,128)}, u32[]{:S(2)}) copy-start(s32[1,128]{1,0:T(1,128)} %param.10) | copy-start | bytes 1540
  21.1 11.1 %copy-start.1 = (f32[1,128,1024]{2,1,0:T(8,128)S(1)}, f32[1,128,1024]{2,1,0:T(8,128)}, u32[]{:S(2)}) copy-start(f32[1,128,1024]{2,1,0:T(8,128)} %param.9) | copy-start | bytes 1572868
  21.1 13.9 %copy-start.2 = (bf16[1,128,1024]{2,1,0:T(8,128)(2,1)S(1)}, bf16[1,128,1024]{2,1,0:T(8,128)(2,1)}, u32[]{:S(2)}) copy-start(bf16[1,128,1024]{2,1,0:T(8,128)(2,1)} %param.13) | copy-start | bytes 786436
  21.1 14.1 %copy-start.17 = (f32[3,1024]{1,0:T(4,128)S(1)}, f32[3,1024]{1,0:T(4,128)}, u32[]{:S(2)}) copy-start(f32[3,1024]{1,0:T(4,128)} %param.12) | copy-start | bytes 36868
  21.1 14.1 %copy-start.18 = (f32[3,1024]{1,0:T(4,128)S(1)}, f32[3,1024]{1,0:T(4,128)}, u32[]{:S(2)}) copy-start(f32[3,1024]{1,0:T(4,128)} %param.11) | copy-start | bytes 36868
  21.1 144.7 %all-to-all-start.1 = ((bf16[8,384,1024]{2,1,0:T(8,128)(2,1)}), bf16[8,384,1024]{2,1,0:T(8,128)(2,1)}, u32[]{:S(2)}, u32[]{:S(2)}) async-start(bf16[8,384,1024]{2,1,0:T(8,128)(2,1)} %stack.32), calls=%async_computation.1 | async-start | bytes 12582912 | tf_op jit(solution)/shard_map/all_to_all | solution.py:28
  27.7 141.9 %collective-permute-start = (f32[1]{0:T(128)}, f32[1]{0:T(128)}, u32[]{:S(2)}, u32[]{:S(2)}) collective-permute-start(f32[1]{0:T(128)} %bitcast.6), channel_id=1, source_target_pairs={{0,4},{4,8},{8,12},{12,16},{16,20},{20,24},{24,28},{1,5},{5,9},{9,... | collective-permute-start | bytes 20 | tf_op jit(solution)/shard_map/ppermute | solution.py:11
  32.1 143.7 %collective-permute-start.1 = (f32[1,1024]{1,0:T(1,128)S(1)}, f32[1,1024]{1,0:T(1,128)S(1)}, u32[]{:S(2)}, u32[]{:S(2)}) collective-permute-start(f32[1,1024]{1,0:T(1,128)S(1)} %slice_bitcast_fusion.1), channel_id=1, source_target_pairs={{0,4},{4,8},{8,12},{12,16},{16,20},{20,24},{24,28},{1,5},{5,9},{9,... | collective-permute-start | bytes 12296 | tf_op jit(solution)/shard_map/ppermute | solution.py:11
  35.2 140.7 %copy-start.3 = (f32[1,1024]{1,0:T(1,128)}, f32[1,1024]{1,0:T(1,128)S(1)}, u32[]{:S(2)}) copy-start(f32[1,1024]{1,0:T(1,128)S(1)} %get-tuple-element.25) | copy-start | bytes 12292
  35.2 140.7 %copy-start.5 = (f32[1,1024]{1,0:T(1,128)}, f32[1,1024]{1,0:T(1,128)S(1)}, u32[]{:S(2)}) copy-start(f32[1,1024]{1,0:T(1,128)S(1)} %get-tuple-element.26) | copy-start | bytes 12292
  35.2 140.7 %copy-start.7 = (f32[1,1024]{1,0:T(1,128)}, f32[1,1024]{1,0:T(1,128)S(1)}, u32[]{:S(2)}) copy-start(f32[1,1024]{1,0:T(1,128)S(1)} %get-tuple-element.27) | copy-start | bytes 12292
  35.2 140.7 %copy-start.9 = (f32[1,1024]{1,0:T(1,128)}, f32[1,1024]{1,0:T(1,128)S(1)}, u32[]{:S(2)}) copy-start(f32[1,1024]{1,0:T(1,128)S(1)} %get-tuple-element.22) | copy-start | bytes 12292
  35.3 140.7 %copy-start.11 = (f32[1,1024]{1,0:T(1,128)}, f32[1,1024]{1,0:T(1,128)S(1)}, u32[]{:S(2)}) copy-start(f32[1,1024]{1,0:T(1,128)S(1)} %get-tuple-element.23) | copy-start | bytes 12292
  35.3 140.7 %copy-start.13 = (f32[1,1024]{1,0:T(1,128)}, f32[1,1024]{1,0:T(1,128)S(1)}, u32[]{:S(2)}) copy-start(f32[1,1024]{1,0:T(1,128)S(1)} %get-tuple-element.24) | copy-start | bytes 12292
  165.8 18.3 %all-to-all-start = ((f32[8,128,128]{2,1,0:T(8,128)}), f32[8,128,128]{2,1,0:T(8,128)S(1)}, u32[]{:S(2)}, u32[]{:S(2)}) async-start(f32[8,128,128]{2,1,0:T(8,128)} %bitcast.2), calls=%async_computation | async-start | bytes 1048576 | tf_op jit(solution)/shard_map/all_to_all | solution.py:54
  170.9 5.1 copy-start.19
  175.9 8.2 %copy-start.15 = (f32[1,1024]{1,0:T(1,128)}, f32[1,1024]{1,0:T(1,128)S(1)}, u32[]{:S(2)}) copy-start(f32[1,1024]{1,0:T(1,128)S(1)} %collective-permute-done.1) | copy-start | bytes 12292
  184.1 18.4 %all-to-all-start.2 = ((f32[8,128,128]{1,2,0:T(8,128)}), f32[8,128,128]{1,2,0:T(8,128)}, u32[]{:S(2)}, u32[]{:S(2)}) async-start(f32[8,128,128]{1,2,0:T(8,128)} %copy_bitcast_fusion), calls=%async_computation.2 | async-start | bytes 1048576 | tf_op jit(solution)/shard_map/all_to_all | solution.py:53
  188.3 297.5 %reduce-scatter.3.cloned.1.call-start = ((), (), s32[]{:S(2)}) async-start(), calls=%async_computation.6 | async-start | bytes 14155776 | tf_op jit(solution)/shard_map/reduce_scatter | solution.py:66
  233.2 11.9 %copy-start.23 = (f32[128,1]{0,1:T(1,128)S(1)}, f32[128,1]{0,1:T(1,128)}, u32[]{:S(2)}) copy-start(f32[128,1]{0,1:T(1,128)} %slice.423) | copy-start | bytes 1540
  242.0 5.8 %copy-start.22 = (f32[128,1]{0,1:T(1,128)S(1)}, f32[128,1]{0,1:T(1,128)}, u32[]{:S(2)}) copy-start(f32[128,1]{0,1:T(1,128)} %slice.422) | copy-start | bytes 1540
  246.8 1.8 copy-start.21
  249.7 22.4 %copy-start.4 = (f32[1,1024]{1,0:T(1,128)S(1)}, f32[1,1024]{1,0:T(1,128)}, u32[]{:S(2)}) copy-start(f32[1,1024]{1,0:T(1,128)} %copy-done.3) | copy-start | bytes 12292
  249.7 22.4 %copy-start.6 = (f32[1,1024]{1,0:T(1,128)S(1)}, f32[1,1024]{1,0:T(1,128)}, u32[]{:S(2)}) copy-start(f32[1,1024]{1,0:T(1,128)} %copy-done.5) | copy-start | bytes 12292
  249.7 22.4 %copy-start.8 = (f32[1,1024]{1,0:T(1,128)S(1)}, f32[1,1024]{1,0:T(1,128)}, u32[]{:S(2)}) copy-start(f32[1,1024]{1,0:T(1,128)} %copy-done.7) | copy-start | bytes 12292
  249.7 22.4 %copy-start.10 = (f32[1,1024]{1,0:T(1,128)S(1)}, f32[1,1024]{1,0:T(1,128)}, u32[]{:S(2)}) copy-start(f32[1,1024]{1,0:T(1,128)} %copy-done.9) | copy-start | bytes 12292
  249.7 22.4 %copy-start.12 = (f32[1,1024]{1,0:T(1,128)S(1)}, f32[1,1024]{1,0:T(1,128)}, u32[]{:S(2)}) copy-start(f32[1,1024]{1,0:T(1,128)} %copy-done.11) | copy-start | bytes 12292
  249.7 22.4 %copy-start.14 = (f32[1,1024]{1,0:T(1,128)S(1)}, f32[1,1024]{1,0:T(1,128)}, u32[]{:S(2)}) copy-start(f32[1,1024]{1,0:T(1,128)} %copy-done.13) | copy-start | bytes 12292
  249.8 22.4 %copy-start.16 = (f32[1,1024]{1,0:T(1,128)S(1)}, f32[1,1024]{1,0:T(1,128)}, u32[]{:S(2)}) copy-start(f32[1,1024]{1,0:T(1,128)} %copy-done.15) | copy-start | bytes 12292
  249.8 22.4 %copy-start.20 = (f32[128]{0:T(128)S(1)}, f32[128]{0:T(128)}, u32[]{:S(2)}) copy-start(f32[128]{0:T(128)} %copy-done.19) | copy-start | bytes 1540
  279.5 253.3 %reduce-scatter.5.cloned.1.call-start = ((), (), s32[]{:S(2)}) async-start(), calls=%async_computation.7 | async-start | bytes 983040 | tf_op jit(solution)/shard_map/reduce_scatter | solution.py:75
Sparse Core Ops, SparseCore 0:
  279.6 206.0 reduce-scatter.2
  488.3 22.2 reduce-scatter.4
